TPU v7x, 32 devices: a whole 2x2x4 slice. The times are simulated.
32 devices in a mesh: grp: 4 (over z), kv: 4 (over y, x), tp: 2 (over core).
Axes of the slice: x: 2, y: 2, z: 4, core: 2. Of those that a mesh axis runs over, the one named last changes fastest.
Arguments:
- hidden_states: bfloat16 [512, 4096], P('grp', 'kv'), may hold values from -6 to 6
- attn_gain: float32 [4096], P('kv'), may hold values from 0.25 to 1.75
- mlp_gain: float32 [4096], replicated, may hold values from 0.25 to 1.75
- w_query: bfloat16 [4096, 4096], P('kv', 'tp'), may hold values from -0.09375 to 0.09375
- w_out: bfloat16 [32, 128, 4096], P('tp', 'kv'), may hold values from -1 to 1
- w_gate: bfloat16 [4096, 14336], P(None, ('kv', 'tp')), may hold values from -0.09375 to 0.09375
- w_up: bfloat16 [4096, 14336], P(None, ('kv', 'tp')), may hold values from -0.09375 to 0.09375
- w_down: bfloat16 [14336, 4096], P(('kv', 'tp')), may hold values from -0.046875 to 0.046875
- kv_pool: bfloat16 [256, 2, 128, 1024], P(('grp', 'kv'), None, None, 'tp'), may hold values from -110 to 110
- resident_cache: bfloat16 [4, 32, 2, 128, 1024], P('grp', 'kv', None, None, 'tp'), may hold values from -110 to 110
- resident_slot: int32 [4, 32], P('grp', 'kv'), may hold values from 0 to 127
- resident_len: int32 [4, 32], P('grp', 'kv'), may hold values from 1 to 128
- new_owner: int32 [4, 64], replicated, may hold values from 0 to 15, as said below
- new_local: int32 [4, 64], replicated, may hold values from 0 to 15
- new_slot: int32 [4, 64], P('grp', 'kv'), may hold values from 0 to 127
- new_len: int32 [4, 64], P('grp', 'kv'), may hold values from 1 to 128
- token_kv: bfloat16 [512, 2, 1024], P('grp', None, 'tp'), may hold values from -6 to 6
Outputs:
- mixed: bfloat16 [512, 4096], P(('grp', 'kv', 'tp'))
- new_cache: bfloat16 [4, 64, 2, 128, 1024], P('grp', 'kv', None, None, 'tp')
Inputs may be any that keep to these rules, and one draw needn't show every extreme that they name: New page c of group g is kept by the device of kv index c // 16 of group g and comes from the device whose index along grp+kv is new_owner[g, c]; every decode device receives exactly 4 new pages from the owners of each grp index; no owner sends more than 4 pages to the devices of one kv index over all groups, so at most 4 to one device; every owner sends each of its 16 pages exactly once.
All inputs are finite; a program needn't handle non-finite values.
Results may differ from a plain program's by a relative error of at most 0.018.
Values may be sent and summed in bfloat16 or wider, within the bound.
No kernel may reach another device: no remote copies, remote signals or barrier semaphores. Data moves between devices by JAX's collectives and lax.ppermute only.
A program may use at most 128 MiB of HBM per device.

v0:
```python
import jax
import jax.numpy as jnp
from jax import lax
from jax.sharding import PartitionSpec as P

D = 4096
HEADS = 32
KV_HEADS = 8
HEAD_DIM = 128
NPR = 4
neg_fill = -1e30
norm_eps = 1e-05


def combined_all(part, axis, combine):
    gathered = jax.tree.map(lambda a: lax.all_gather(a, axis), part)

    def take(source):
        return jax.tree.map(lambda a: lax.dynamic_index_in_dim(a, source, 0, False), gathered)

    return lax.fori_loop(
        1, lax.axis_size(axis), lambda source, state: combine(state, take(source)), take(0)
    )


def combine(earlier, later):
    top_a, sum_a, acc_a = earlier
    top_b, sum_b, acc_b = later
    top = jnp.maximum(top_a, top_b)
    fade_a = jnp.exp(top_a - top)
    fade_b = jnp.exp(top_b - top)
    return (
        top,
        sum_a * fade_a + sum_b * fade_b,
        acc_a * fade_a[..., None] + acc_b * fade_b[..., None],
    )


def nth_match(table, wanted, places):
    matched = (table == wanted).astype(jnp.int32)
    ranking = jnp.cumsum(matched, axis=1) - 1
    return (matched[:, None, :] == 1) & (ranking[:, None, :] == places[None, :, None])


def move_pages(kv_pool, new_owner, new_local):
    groups = lax.axis_size("grp")
    ranks = lax.axis_size("kv")
    per_dev = new_owner.shape[1] // ranks
    cap = groups * NPR // ranks
    grp_rank = lax.axis_index("grp")
    kv_rank = lax.axis_index("kv")
    owners = new_owner.reshape(groups * ranks, per_dev)
    myself = grp_rank * ranks + kv_rank
    places = jnp.arange(cap, dtype=jnp.int32)
    mine = lax.dynamic_index_in_dim(owners, myself, 0, keepdims=False)
    order = jnp.arange(per_dev, dtype=jnp.int32)
    by_col = (
        new_owner.reshape(groups, ranks, per_dev)
        .transpose(1, 0, 2)
        .reshape(ranks, groups * per_dev)
    )
    local_col = (
        new_local.reshape(groups, ranks, per_dev)
        .transpose(1, 0, 2)
        .reshape(ranks, groups * per_dev)
    )
    select = nth_match(by_col, myself, places)
    picked = jnp.sum(jnp.where(select, local_col[:, None, :], 0), axis=2)
    outgoing = jnp.take(kv_pool, picked.reshape(-1), axis=0)
    received = lax.all_to_all(outgoing, "kv", split_axis=0, concat_axis=0, tiled=True)
    row_here = lax.dynamic_index_in_dim(by_col, kv_rank, 0, keepdims=False)
    sources = grp_rank * ranks + jnp.arange(ranks, dtype=jnp.int32)
    hits = nth_match(
        jnp.broadcast_to(row_here[None, :], (ranks, row_here.shape[0])), sources[:, None], places
    )
    spots = jnp.arange(row_here.shape[0], dtype=jnp.int32)
    where_f = jnp.sum(jnp.where(hits, spots[None, None, :], 0), axis=2).reshape(-1)
    dest_grp = where_f // per_dev
    dest_pos = where_f % per_dev
    same = (dest_grp[:, None] == dest_grp[None, :]) & (dest_pos[:, None] < dest_pos[None, :])
    rank_in = jnp.sum(same.astype(jnp.int32), axis=0)
    target = dest_grp * NPR + rank_in
    items = jnp.arange(target.shape[0], dtype=jnp.int32)
    inverse = jnp.sum(jnp.where(target[None, :] == items[:, None], items[None, :], 0), axis=1)
    sorted_pages = jnp.take(received, inverse, axis=0)
    arrived = lax.all_to_all(sorted_pages, "grp", split_axis=0, concat_axis=0, tiled=True)
    src_grp = mine // ranks
    earlier = (src_grp[:, None] == src_grp[None, :]) & (order[:, None] < order[None, :])
    before = jnp.sum(earlier.astype(jnp.int32), axis=0)
    return jnp.take(arrived, src_grp * NPR + before, axis=0)


def local_partials(query, resident, arrived, res_slot, res_len, arr_slot, arr_len, token_kv, first):
    pages = jnp.concatenate([resident, arrived], axis=0)
    owner_slot = jnp.concatenate([res_slot, arr_slot])
    filled = jnp.concatenate([res_len, arr_len])
    count = pages.shape[0]
    tokens = pages.shape[2]
    kv_here = pages.shape[3] // HEAD_DIM
    slots = query.shape[0]
    ratio = HEADS // KV_HEADS
    keys = pages[:, 0].astype(jnp.float32).reshape(count, tokens, kv_here, HEAD_DIM)
    values = pages[:, 1].astype(jnp.float32).reshape(count, tokens, kv_here, HEAD_DIM)
    grouped = query.reshape(slots, kv_here, ratio, HEAD_DIM)
    picked = jnp.take(grouped, owner_slot, axis=0)
    scores = jnp.einsum("ikgd,itkd->ikgt", picked, keys, precision=lax.Precision.HIGHEST)
    usable = (jnp.arange(tokens, dtype=jnp.int32)[None, :] < filled[:, None])[:, None, None, :]
    scores = jnp.where(usable, scores, neg_fill)
    page_top = jnp.max(scores, axis=3)
    member = owner_slot[None, :] == jnp.arange(slots, dtype=jnp.int32)[:, None]
    slot_top = jnp.max(jnp.where(member[:, :, None, None], page_top[None], neg_fill), axis=1)
    own_keys = token_kv[:, 0].astype(jnp.float32).reshape(slots, kv_here, HEAD_DIM)
    own_values = token_kv[:, 1].astype(jnp.float32).reshape(slots, kv_here, HEAD_DIM)
    own_score = jnp.einsum("skgd,skd->skg", grouped, own_keys, precision=lax.Precision.HIGHEST)
    own_score = jnp.where(first, own_score, neg_fill)
    slot_top = jnp.maximum(slot_top, own_score)
    reach = jnp.take(slot_top, owner_slot, axis=0)
    weights = jnp.where(usable, jnp.exp(scores - reach[..., None]), 0.0)
    page_sum = jnp.sum(weights, axis=3)
    page_acc = jnp.einsum("ikgt,itkd->ikgd", weights, values, precision=lax.Precision.HIGHEST)
    own_weight = jnp.where(first, jnp.exp(own_score - slot_top), 0.0)
    member_f = member.astype(jnp.float32)
    total = jnp.dot(member_f, page_sum.reshape(count, -1), precision=lax.Precision.HIGHEST)
    total = total + own_weight.reshape(slots, -1)
    weighted = jnp.dot(member_f, page_acc.reshape(count, -1), precision=lax.Precision.HIGHEST)
    weighted = (
        weighted.reshape(slots, kv_here, ratio, HEAD_DIM)
        + own_weight[..., None] * own_values[:, :, None, :]
    )
    return (slot_top.reshape(slots, -1), total, weighted.reshape(slots, kv_here * ratio, HEAD_DIM))


def per_device(
    hidden_states,
    attn_gain,
    mlp_gain,
    w_query,
    w_out,
    w_gate,
    w_up,
    w_down,
    kv_pool,
    resident_cache,
    resident_slot,
    resident_len,
    new_owner,
    new_local,
    new_slot,
    new_len,
    token_kv,
):
    ranks = lax.axis_size("kv")
    pairs = lax.axis_size("tp")
    kv_rank = lax.axis_index("kv")
    tp_rank = lax.axis_index("tp")
    features = hidden_states.astype(jnp.float32)
    partial_query = jnp.dot(
        (features * attn_gain).astype(jnp.bfloat16), w_query, preferred_element_type=jnp.float32
    )
    squares = jnp.sum(features * features, axis=1)
    partial_query, squares = lax.psum((partial_query, squares), "kv")
    attn_scale = lax.rsqrt(squares / D + norm_eps)
    query = partial_query * attn_scale[:, None] * HEAD_DIM ** (-0.5)
    new_pages = move_pages(kv_pool, new_owner, new_local)
    top, total, weighted = local_partials(
        query,
        resident_cache[0],
        new_pages,
        resident_slot[0],
        resident_len[0],
        new_slot[0],
        new_len[0],
        token_kv,
        kv_rank == 0,
    )
    top, total, weighted = combined_all((top, total, weighted), "kv", combine)
    attn = (weighted / total[..., None]).astype(jnp.bfloat16)
    slots = attn.shape[0]
    heads_here = attn.shape[1]
    span = HEAD_DIM // ranks
    piece = lax.dynamic_slice_in_dim(attn, kv_rank * span, span, 2)
    branch = jnp.dot(
        piece.reshape(slots, heads_here * span),
        w_out.reshape(heads_here * span, w_out.shape[2]),
        preferred_element_type=jnp.float32,
    )
    width_here = hidden_states.shape[1]
    laid = branch.reshape(slots, ranks, width_here)
    spot = (jnp.arange(ranks, dtype=jnp.int32) == kv_rank) & (tp_rank == 0)
    laid = laid + jnp.where(spot[None, :, None], features[:, None, :], 0.0)
    resid = lax.psum(laid.reshape(slots, ranks * width_here).astype(jnp.bfloat16), ("kv", "tp"))
    resid_f = resid.astype(jnp.float32)
    mlp_scale = lax.rsqrt(jnp.sum(resid_f * resid_f, axis=1) / D + norm_eps)
    normed_mlp = (resid_f * mlp_gain).astype(jnp.bfloat16)
    gate = jnp.dot(normed_mlp, w_gate, preferred_element_type=jnp.float32) * mlp_scale[:, None]
    upward = jnp.dot(normed_mlp, w_up, preferred_element_type=jnp.float32) * mlp_scale[:, None]
    hidden_units = (jax.nn.silu(gate) * upward).astype(jnp.bfloat16)
    row_count = slots // (ranks * pairs)
    down = lax.psum_scatter(
        jnp.dot(hidden_units, w_down, preferred_element_type=jnp.float32).astype(jnp.bfloat16),
        ("kv", "tp"),
        scatter_dimension=0,
        tiled=True,
    ).astype(jnp.float32)
    row_start = (kv_rank * pairs + tp_rank) * row_count
    kept = lax.dynamic_slice_in_dim(resid_f, row_start, row_count, 0)
    mixed = (kept + down).astype(jnp.bfloat16)
    return (mixed, new_pages[None])


def solution(mesh):
    return jax.shard_map(
        per_device,
        mesh=mesh,
        in_specs=(
            P("grp", "kv"),
            P("kv"),
            P(),
            P("kv", "tp"),
            P("tp", "kv", None),
            P(None, ("kv", "tp")),
            P(None, ("kv", "tp")),
            P(("kv", "tp"), None),
            P(("grp", "kv"), None, None, "tp"),
            P("grp", "kv", None, None, "tp"),
            P("grp", "kv"),
            P("grp", "kv"),
            P(),
            P(),
            P("grp", "kv"),
            P("grp", "kv"),
            P("grp", None, "tp"),
        ),
        out_specs=(P(("grp", "kv", "tp"), None), P("grp", "kv", None, None, "tp")),
        check_vma=False,
    )
```

profile of v0, /device:TPU:0, one launch (start us, length us, event | category | flops | bytes accessed | tf_op | source)
XLA Modules:
  0.0 407.0 jit_solution(611504076523170792)
XLA Ops:
  7.2 0.8 reshape.445
  7.9 0.8 reshape.450
  9.0 0.8 reshape.447
  10.2 5.0 %gather_fusion.2 = bf16[16,2,128,512]{3,2,1,0:T(8,128)(2,1)} fusion(bf16[16,2,128,512]{3,2,1,0:T(8,128)(2,1)} %param.29, s32[1024]{0:T(1024)S(1)} %pad_clamp_fusion.2), kind=kCustom, calls=%fused_computation.clone | custom fusion | bytes 8388672 | tf_op jit(solution)/shard_map/jit(_take)/gather | solution.py:69
  15.2 4.7 %broadcast_select_fusion.2 = bf16[16,2,128,512]{3,2,1,0:T(8,128)(2,1)} fusion(bf16[16,2,128,512]{3,2,1,0:T(8,128)(2,1)} %gather_fusion.2, pred[16]{0:T(512)(128)(4,1)S(1)} %compare_and_fusion.2), kind=kLoop, calls=%fused_computation.18 | loop fusion | flops 2097152 | bytes 8388624 | tf_op jit(solution)/shard_map/jit(_take)/select_n | solution.py:69
  19.9 5.2 %all-to-all-start = ((bf16[16,2,128,512]{3,2,1,0:T(8,128)(2,1)}), bf16[16,2,128,512]{3,2,1,0:T(8,128)(2,1)}, u32[]{:S(2)}, u32[]{:S(2)}) async-start(bf16[16,2,128,512]{3,2,1,0:T(8,128)(2,1)} %broadcast_select_fusion.2), calls=%async_computation | async-start | bytes 8388608 | tf_op jit(solution)/shard_map/all_to_all | solution.py:70
  25.9 47.8 %all-to-all-done = bf16[16,2,128,512]{3,2,1,0:T(8,128)(2,1)} async-done(((bf16[16,2,128,512]{3,2,1,0:T(8,128)(2,1)}), bf16[16,2,128,512]{3,2,1,0:T(8,128)(2,1)}, u32[]{:S(2)}, u32[]{:S(2)}) %all-to-all-start) | async-done | bytes 4194336 | tf_op jit(solution)/shard_map/all_to_all | solution.py:70
  73.7 5.0 %gather_fusion.3 = bf16[16,2,128,512]{3,2,1,0:T(8,128)(2,1)} fusion(bf16[16,2,128,512]{3,2,1,0:T(8,128)(2,1)} %all-to-all-done, s32[1024]{0:T(1024)S(1)} %pad_clamp_fusion.1), kind=kCustom, calls=%fused_computation.1.clone | custom fusion | bytes 8388672 | tf_op jit(solution)/shard_map/jit(_take)/gather | solution.py:85
  78.7 4.7 %broadcast_select_fusion.1 = bf16[16,2,128,512]{3,2,1,0:T(8,128)(2,1)} fusion(bf16[16,2,128,512]{3,2,1,0:T(8,128)(2,1)} %gather_fusion.3, pred[16]{0:T(512)(128)(4,1)S(1)} %compare_and_fusion.1), kind=kLoop, calls=%fused_computation.17 | loop fusion | flops 2097152 | bytes 8388624 | tf_op jit(solution)/shard_map/jit(_take)/select_n | solution.py:85
  83.4 5.2 %all-to-all-start.1 = ((bf16[16,2,128,512]{3,2,1,0:T(8,128)(2,1)}), bf16[16,2,128,512]{3,2,1,0:T(8,128)(2,1)}, u32[]{:S(2)}, u32[]{:S(2)}) async-start(bf16[16,2,128,512]{3,2,1,0:T(8,128)(2,1)} %broadcast_select_fusion.1), calls=%async_computation.1 | async-start | bytes 8388608 | tf_op jit(solution)/shard_map/all_to_all | solution.py:86
  88.7 4.0 fusion.7
  93.9 0.7 copy.134
  94.6 9.3 %psum.22 = f32[128]{0:T(128)S(1)} all-reduce(f32[128]{0:T(128)S(1)} %multiply_reduce_fusion.1), channel_id=1, replica_groups=mesh['grp'=4,'kv'=4,'tp'=2] {'kv'}, use_global_device_ids=true, to_apply=%region_2.0 | all-reduce | flops 128 | bytes 1024 | tf_op jit(solution)/shard_map/psum | solution.py:161
  104.2 41.8 %all-reduce.3.cloned.1.call-done = f32[128,2048]{1,0:T(8,128)} async-done(((f32[128,2048]{1,0:T(8,128)}), f32[128,2048]{1,0:T(8,128)}) %all-reduce.3.cloned.1.call-update) | async-done | bytes 1048592 | tf_op jit(solution)/shard_map/psum | solution.py:161
  145.9 1.4 multiply_multiply_fusion
  148.0 1.3 gather_fusion
  149.4 2.5 fusion.34
  151.9 29.4 %all-to-all-done.1 = bf16[16,2,128,512]{3,2,1,0:T(8,128)(2,1)} async-done(((bf16[16,2,128,512]{3,2,1,0:T(8,128)(2,1)}), bf16[16,2,128,512]{3,2,1,0:T(8,128)(2,1)}, u32[]{:S(2)}, u32[]{:S(2)}) %all-to-all-start.1) | async-done | bytes 4194336 | tf_op jit(solution)/shard_map/all_to_all | solution.py:86
  181.3 5.0 %gather_fusion.4 = bf16[16,2,128,512]{3,2,1,0:T(8,128)(2,1)} fusion(bf16[16,2,128,512]{3,2,1,0:T(8,128)(2,1)} %all-to-all-done.1, s32[1024]{0:T(1024)S(1)} %pad_clamp_fusion), kind=kCustom, calls=%fused_computation.2.clone | custom fusion | bytes 8388672 | tf_op jit(solution)/shard_map/jit(_take)/gather | solution.py:90
  186.3 2.8 broadcast_select_fusion
  189.1 2.9 pad_maximum_fusion
  192.0 3.5 copy.122
  195.5 4.2 %fusion.33 = (f32[24,4,4]{2,1,0:T(4,128)S(1)}, f32[24,4,4,128]{3,2,1,0:T(4,128)}) fusion(bf16[24,128,4,128]{1,3,2,0:T(8,128)(2,1)S(1)} %bitcast.91, f32[24,4,4,128]{3,2,1,0:T(4,128)} %gather_fusion, pred[24]{0:T(512)(128)(4,1)S(1)} %get-tuple-element.244, pred[24,128]{1,0:T(8,128)(4,1)S(1)} %iota_compare_fusion), kind=kOutput, calls=%fused_computation.125 | convolution fusion | flops 75644544 | bytes 3543576 | tf_op jit(solution)/shard_map/ikgd,itkd->ikgt/dot_general | solution.py:106
  200.2 1.8 exponential_select_fusion
  202.7 3.5 copy.130
  206.2 6.6 %fusion.13 = f32[24,4,4,128]{3,2,1,0:T(4,128)} fusion(bf16[24,128,4,128]{1,3,2,0:T(8,128)(2,1)S(1)} %bitcast.95, f32[24,4,4,128]{3,2,1,0:T(4,128)} %get-tuple-element.261, f32[24,4,4]{2,1,0:T(4,128)S(1)} %broadcast_select_fusion.3, pred[24,128]{1,0:T(8,128)(4,1)S(1)} %iota_compare_fusion), kind=kOutput, calls=%fused_computation.50 | convolution fusion | flops 75595776 | bytes 3543552 | tf_op jit(solution)/shard_map/ikgt,itkd->ikgd/dot_general | solution.py:120
  212.8 1.0 reshape.456
  214.0 1.0 copy.129
  215.0 1.7 convolution_add_fusion
  216.8 1.7 copy.135
  218.8 6.7 %copy.138 = bf16[4096,512]{1,0:T(8,128)(2,1)} copy(bf16[4096,512]{0,1:T(8,128)(2,1)} %bitcast.92) | data formatting | bytes 8388608 | tf_op jit(solution)/shard_map/dot_general | solution.py:182
  226.2 8.0 %all-gather = f32[512,16]{0,1:T(8,128)S(1)} all-gather(f32[128,16]{0,1:T(8,128)S(1)} %convolution_add_fusion.1), channel_id=2, replica_groups=mesh['grp'=4,'kv'=4,'tp'=2] {'kv'}, dimensions={0}, use_global_device_ids=true | all-gather | bytes 40960 | tf_op jit(solution)/shard_map/all_gather | solution.py:16
  234.3 8.2 %all_gather.12 = f32[4,128,16]{1,2,0:T(8,128)S(1)} all-gather(f32[1,128,16]{1,2,0:T(8,128)S(1)} %bitcast.104), channel_id=1, replica_groups=mesh['grp'=4,'kv'=4,'tp'=2] {'kv'}, dimensions={0}, use_global_device_ids=true | all-gather | bytes 40960 | tf_op jit(solution)/shard_map/all_gather | solution.py:16
  242.5 26.1 %all-gather.3.cloned.1.call-done = f32[4,128,16,128]{3,2,1,0:T(8,128)} async-done(((f32[1,128,16,128]{3,2,1,0:T(8,128)}), f32[4,128,16,128]{3,2,1,0:T(8,128)}) %all-gather.3.cloned.1.call-update) | async-done | bytes 4194320 | tf_op jit(solution)/shard_map/all_gather | solution.py:16
  268.7 1.3 slice_bitcast_fusion
  270.0 6.5 %while.19 = (s32[]{:T(128)}, f32[128,16]{0,1:T(8,128)S(1)}, f32[128,16]{0,1:T(8,128)S(1)}, f32[128,16,128]{2,1,0:T(8,128)S(1)}, f32[4,128,16]{1,2,0:T(8,128)S(1)...) while((s32[]{:T(128)}, f32[128,16]{0,1:T(8,128)S(1)}, ...), condition=%wide.region_14.16_spmd, body=%wide.region_13.15_spmd.sunk | while | flops 798725 | bytes 3276955 | solution.py:21
  270.2 1.9 fusion.48
  272.4 1.9 fusion.48
  274.5 1.9 fusion.48
  276.9 3.7 add_convert_fusion
  281.3 1.4 copy.141
  282.7 56.8 %all-reduce.5.cloned.1.call-done = bf16[128,4096]{1,0:T(8,128)(2,1)} async-done(((bf16[128,4096]{1,0:T(8,128)(2,1)}), bf16[128,4096]{1,0:T(8,128)(2,1)}) %all-reduce.5.cloned.1.call-update) | async-done | bytes 1048592 | tf_op jit(solution)/shard_map/psum | solution.py:191
  339.6 1.5 multiply_reduce_fusion
  341.1 7.7 %convolution_multiply_fusion.1 = f32[128,1792]{1,0:T(8,128)S(1)} fusion(bf16[4096,1792]{1,0:T(8,128)(2,1)} %param.26, f32[4096]{0:T(1024)S(1)} %copy-done.7, bf16[128,4096]{1,0:T(8,128)(2,1)} %all-reduce.5.cloned.1.call-done, f32[128]{0:T(128)S(1)} %add_rsqrt_fusion), kind=kOutput, calls=%fused_computation.22 | convolution fusion | flops 1880850432 | bytes 16663040 | tf_op jit(solution)/shard_map/dot_general | solution.py:195
  348.8 14.8 %convolution_convert_fusion = bf16[128,4096]{1,0:T(8,128)(2,1)} fusion(bf16[1792,4096]{1,0:T(8,128)(2,1)} %param.28, bf16[4096,1792]{1,0:T(8,128)(2,1)} %param.27, f32[128,1792]{1,0:T(8,128)S(1)} %convolution_multiply_fusion.1, f32[4096]{0:T(1024)S(1)} %copy-done.7, bf16[128,4096]{1,0:T(8,128)(2,1)S(1)} %copy-done, f32[128]{0:T(128)S(1)} %add_rsqrt_fusion), kind=kOutput, calls=%fused_computation.15 | convolution fusion | flops 3761799168 | bytes 32391680 | tf_op jit(solution)/shard_map/dot_general | solution.py:200
  363.6 4.7 %fusion.46 = bf16[1,16,2,128,512]{4,3,2,1,0:T(8,128)(2,1)} fusion(bf16[16,2,128,512]{3,2,1,0:T(8,128)(2,1)} %gather_fusion.4, pred[16]{0:T(512)(128)(4,1)S(1)} %get-tuple-element.246), kind=kLoop, calls=%fused_computation.127 | loop fusion | flops 2097152 | bytes 8388624 | tf_op jit(solution)/shard_map/broadcast_in_dim | solution.py:208
  368.4 30.5 %reduce-scatter.2.cloned.1.call-done = bf16[16,4096]{1,0:T(8,128)(2,1)} async-done(((bf16[128,4096]{1,0:T(8,128)(2,1)}), bf16[16,4096]{1,0:T(8,128)(2,1)}) %reduce-scatter.2.cloned.1.call-update) | async-done | bytes 131088 | tf_op jit(solution)/shard_map/reduce_scatter | solution.py:199
  398.9 1.6 add_convert_fusion.1
  (108 shorter events, 8.3 us)
Async XLA Ops:
  19.9 53.8 %all-to-all-start = ((bf16[16,2,128,512]{3,2,1,0:T(8,128)(2,1)}), bf16[16,2,128,512]{3,2,1,0:T(8,128)(2,1)}, u32[]{:S(2)}, u32[]{:S(2)}) async-start(bf16[16,2,128,512]{3,2,1,0:T(8,128)(2,1)} %broadcast_select_fusion.2), calls=%async_computation | async-start | bytes 8388608 | tf_op jit(solution)/shard_map/all_to_all | solution.py:70
  83.4 5.3 %copy-start.1 = (bf16[128,1024]{1,0:T(8,128)(2,1)S(1)}, bf16[128,1024]{1,0:T(8,128)(2,1)}, u32[]{:S(2)}) copy-start(bf16[128,1024]{1,0:T(8,128)(2,1)} %param.21) | copy-start | bytes 786436
  83.4 5.3 %copy-start.8 = (f32[1024]{0:T(1024)S(1)}, f32[1024]{0:T(1024)}, u32[]{:S(2)}) copy-start(f32[1024]{0:T(1024)} %param.22) | copy-start | bytes 12292
  83.4 97.9 %all-to-all-start.1 = ((bf16[16,2,128,512]{3,2,1,0:T(8,128)(2,1)}), bf16[16,2,128,512]{3,2,1,0:T(8,128)(2,1)}, u32[]{:S(2)}, u32[]{:S(2)}) async-start(bf16[16,2,128,512]{3,2,1,0:T(8,128)(2,1)} %broadcast_select_fusion.1), calls=%async_computation.1 | async-start | bytes 8388608 | tf_op jit(solution)/shard_map/all_to_all | solution.py:86
  88.6 4.2 %copy-start.9 = (s32[1,16]{1,0:T(1,128)S(1)}, s32[1,16]{1,0:T(1,128)}, u32[]{:S(2)}) copy-start(s32[1,16]{1,0:T(1,128)} %param.35) | copy-start | bytes 196
  88.6 4.2 %copy-start.10 = (s32[1,8]{1,0:T(1,128)S(1)}, s32[1,8]{1,0:T(1,128)}, u32[]{:S(2)}) copy-start(s32[1,8]{1,0:T(1,128)} %param.31) | copy-start | bytes 100
  88.6 4.5 %copy-start.5 = (bf16[128,2,512]{2,1,0:T(2,128)(2,1)S(1)}, bf16[128,2,512]{2,1,0:T(2,128)(2,1)}, u32[]{:S(2)}) copy-start(bf16[128,2,512]{2,1,0:T(2,128)(2,1)} %param.37) | copy-start | bytes 786436
  88.6 4.9 %copy-start.11 = (s32[1,16]{1,0:T(1,128)S(1)}, s32[1,16]{1,0:T(1,128)}, u32[]{:S(2)}) copy-start(s32[1,16]{1,0:T(1,128)} %param.36) | copy-start | bytes 196
  88.6 4.9 %copy-start.12 = (s32[1,8]{1,0:T(1,128)S(1)}, s32[1,8]{1,0:T(1,128)}, u32[]{:S(2)}) copy-start(s32[1,8]{1,0:T(1,128)} %param.32) | copy-start | bytes 100
  88.6 57.3 %all-reduce.3.cloned.1.call-start = ((), (), s32[]{:S(2)}) async-start(), calls=%async_computation.3 | async-start | bytes 2097152 | tf_op jit(solution)/shard_map/psum | solution.py:161
  92.7 176.0 %all-gather.3.cloned.1.call-start = ((), (), s32[]{:S(2)}) async-start(), calls=%async_computation.4 | async-start | bytes 5242880 | tf_op jit(solution)/shard_map/all_gather | solution.py:16
  186.3 2.9 copy-start.2
  202.0 0.7 copy-start.3
  218.5 121.1 %all-reduce.5.cloned.1.call-start = ((), (), s32[]{:S(2)}) async-start(), calls=%async_computation.5 | async-start | bytes 2097152 | tf_op jit(solution)/shard_map/psum | solution.py:191
  218.8 6.7 %copy-start.6 = (f32[24,4,4,128]{3,2,1,0:T(4,128)S(1)}, f32[24,4,4,128]{3,2,1,0:T(4,128)}, u32[]{:S(2)}) copy-start(f32[24,4,4,128]{3,2,1,0:T(4,128)} %get-tuple-element.261) | copy-start | bytes 589828
  218.8 15.4 %copy-start.4 = (f32[128,4,4]{2,1,0:T(4,128)S(1)}, f32[128,4,4]{2,1,0:T(4,128)}, u32[]{:S(2)}) copy-start(f32[128,4,4]{2,1,0:T(4,128)} %copy-done.3) | copy-start | bytes 24580
  280.6 60.4 %copy-start.7 = (f32[4096]{0:T(1024)S(1)}, f32[4096]{0:T(1024)}, u32[]{:S(2)}) copy-start(f32[4096]{0:T(1024)} %param.23) | copy-start | bytes 49156
  282.7 116.2 %reduce-scatter.2.cloned.1.call-start = ((), (), s32[]{:S(2)}) async-start(), calls=%async_computation.6 | async-start | bytes 1179648 | tf_op jit(solution)/shard_map/reduce_scatter | solution.py:199
  341.1 7.7 %copy-start = (bf16[128,4096]{1,0:T(8,128)(2,1)S(1)}, bf16[128,4096]{1,0:T(8,128)(2,1)}, u32[]{:S(2)}) copy-start(bf16[128,4096]{1,0:T(8,128)(2,1)} %all-reduce.5.cloned.1.call-done) | copy-start | bytes 3145732
Sparse Core Ops, SparseCore 0:
  92.8 53.0 all-reduce.2
  218.6 50.0 all-gather.2
  282.8 56.6 all-reduce.4
  363.7 35.1 reduce-scatter.1
where the time goes:
time: 408 us; the launch traced here: 407 us
  waiting for transfers between devices  232 us (57%)
  matrix products  45.4 us (11%)
  local copies, waits for them, and re-layouts  43.9 us (11%)
  other arithmetic  34.8 us (9%)
  blocking collectives  25.5 us (6%)
  between operations  14.2 us (3%)
  starting transfers between devices  10.8 us (3%)
    psum x1, waiting for transfers between devices, per_device(): lax.psum(laid.reshape(slots, ranks * width_here).astype(jnp.bfloat16), ('...  56.8 us
    all_to_all x1, waiting for transfers between devices, move_pages(): lax.all_to_all(outgoing, 'kv', split_axis=0, concat_axis=0, tiled=True)  47.8 us
    psum x1, waiting for transfers between devices, per_device(): partial_query, squares = lax.psum((partial_query, squares), 'kv')  41.8 us
    reduce_scatter x1, waiting for transfers between devices, per_device(): lax.psum_scatter(jnp.dot(hidden_units, w_down, preferred_element_type=jnp...  30.5 us
    all_to_all x1, waiting for transfers between devices, move_pages(): lax.all_to_all(sorted_pages, 'grp', split_axis=0, concat_axis=0, tiled=True)  29.4 us
    all_gather x1, waiting for transfers between devices, combined_all(): gathered = jax.tree.map(lambda a: lax.all_gather(a, axis), part)  26.1 us
    all_gather x2, blocking collectives, combined_all(): gathered = jax.tree.map(lambda a: lax.all_gather(a, axis), part)  16.2 us
    dot_general x1, matrix products, per_device(): jnp.dot(hidden_units, w_down, preferred_element_type=jnp.float32)  14.8 us
  transfers between devices with their start and end apart: 6, of which 6 were waited for; matrix products, arithmetic and copies ran while one was open for 6% of the time, Pallas kernels for 0%

commit v1 on v0

--- a/solution.py
+++ b/solution.py
@@ -188,7 +188,9 @@
     laid = branch.reshape(slots, ranks, width_here)
     spot = (jnp.arange(ranks, dtype=jnp.int32) == kv_rank) & (tp_rank == 0)
     laid = laid + jnp.where(spot[None, :, None], features[:, None, :], 0.0)
-    resid = lax.psum(laid.reshape(slots, ranks * width_here).astype(jnp.bfloat16), ("kv", "tp"))
+    resid = lax.psum(
+        lax.psum(laid.reshape(slots, ranks * width_here).astype(jnp.bfloat16), "kv"), "tp"
+    )
     resid_f = resid.astype(jnp.float32)
     mlp_scale = lax.rsqrt(jnp.sum(resid_f * resid_f, axis=1) / D + norm_eps)
     normed_mlp = (resid_f * mlp_gain).astype(jnp.bfloat16)

time: 408 us -> 428 us (1.049)
  waiting for transfers between devices: 232 us -> 252 us
    psum x1 -> x2, waiting for transfers between devices: 56.8 us -> 74.2 us  [the longest x1 52.6 us: per_device(): lax.psum(laid.reshape(slots, ranks * width_here).astype(jnp.bfloat16), 'kv')]
  transfers between devices with their start and end apart: 6 -> 7, of which waited for: 6 -> 7; matrix products, arithmetic and copies ran while one was open for 6% -> 6% of each run, Pallas kernels for 0% -> 0%
where the time goes in v1:
time: 428 us; the launch traced here: 426 us
  waiting for transfers between devices  252 us (59%)
  matrix products  45.4 us (11%)
  local copies, waits for them, and re-layouts  43.9 us (10%)
  other arithmetic  34.8 us (8%)
  blocking collectives  25.5 us (6%)
  between operations  14.2 us (3%)
  starting transfers between devices  10.8 us (3%)
    psum x1, waiting for transfers between devices, per_device(): lax.psum(laid.reshape(slots, ranks * width_here).astype(jnp.bfloat16), 'kv')  52.6 us
    all_to_all x1, waiting for transfers between devices, move_pages(): lax.all_to_all(outgoing, 'kv', split_axis=0, concat_axis=0, tiled=True)  47.8 us
    psum x1, waiting for transfers between devices, per_device(): partial_query, squares = lax.psum((partial_query, squares), 'kv')  41.8 us
    reduce_scatter x1, waiting for transfers between devices, per_device(): lax.psum_scatter(jnp.dot(hidden_units, w_down, preferred_element_type=jnp...  32.5 us
    all_to_all x1, waiting for transfers between devices, move_pages(): lax.all_to_all(sorted_pages, 'grp', split_axis=0, concat_axis=0, tiled=True)  29.4 us
    all_gather x1, waiting for transfers between devices, combined_all(): gathered = jax.tree.map(lambda a: lax.all_gather(a, axis), part)  26.1 us
    psum x1, waiting for transfers between devices, per_device(): lax.psum(lax.psum(laid.reshape(slots, ranks * width_here).astype(jnp.bflo...  21.6 us
    all_gather x2, blocking collectives, combined_all(): gathered = jax.tree.map(lambda a: lax.all_gather(a, axis), part)  16.2 us
  transfers between devices with their start and end apart: 7, of which 7 were waited for; matrix products, arithmetic and copies ran while one was open for 6% of the time, Pallas kernels for 0%

profile of v1, /device:TPU:0, one launch (start us, length us, event | category | flops | bytes accessed | tf_op | source)
XLA Modules:
  0.0 426.4 jit_solution(12903447836001095920)
XLA Ops:
  7.2 0.8 reshape.445
  7.9 0.8 reshape.450
  9.0 0.8 reshape.447
  10.2 5.0 %gather_fusion.2 = bf16[16,2,128,512]{3,2,1,0:T(8,128)(2,1)} fusion(bf16[16,2,128,512]{3,2,1,0:T(8,128)(2,1)} %param.29, s32[1024]{0:T(1024)S(1)} %pad_clamp_fusion.2), kind=kCustom, calls=%fused_computation.clone | custom fusion | bytes 8388672 | tf_op jit(solution)/shard_map/jit(_take)/gather | solution.py:69
  15.2 4.7 %broadcast_select_fusion.2 = bf16[16,2,128,512]{3,2,1,0:T(8,128)(2,1)} fusion(bf16[16,2,128,512]{3,2,1,0:T(8,128)(2,1)} %gather_fusion.2, pred[16]{0:T(512)(128)(4,1)S(1)} %compare_and_fusion.2), kind=kLoop, calls=%fused_computation.18 | loop fusion | flops 2097152 | bytes 8388624 | tf_op jit(solution)/shard_map/jit(_take)/select_n | solution.py:69
  19.9 5.2 %all-to-all-start = ((bf16[16,2,128,512]{3,2,1,0:T(8,128)(2,1)}), bf16[16,2,128,512]{3,2,1,0:T(8,128)(2,1)}, u32[]{:S(2)}, u32[]{:S(2)}) async-start(bf16[16,2,128,512]{3,2,1,0:T(8,128)(2,1)} %broadcast_select_fusion.2), calls=%async_computation | async-start | bytes 8388608 | tf_op jit(solution)/shard_map/all_to_all | solution.py:70
  25.9 47.8 %all-to-all-done = bf16[16,2,128,512]{3,2,1,0:T(8,128)(2,1)} async-done(((bf16[16,2,128,512]{3,2,1,0:T(8,128)(2,1)}), bf16[16,2,128,512]{3,2,1,0:T(8,128)(2,1)}, u32[]{:S(2)}, u32[]{:S(2)}) %all-to-all-start) | async-done | bytes 4194336 | tf_op jit(solution)/shard_map/all_to_all | solution.py:70
  73.7 5.0 %gather_fusion.3 = bf16[16,2,128,512]{3,2,1,0:T(8,128)(2,1)} fusion(bf16[16,2,128,512]{3,2,1,0:T(8,128)(2,1)} %all-to-all-done, s32[1024]{0:T(1024)S(1)} %pad_clamp_fusion.1), kind=kCustom, calls=%fused_computation.1.clone | custom fusion | bytes 8388672 | tf_op jit(solution)/shard_map/jit(_take)/gather | solution.py:85
  78.7 4.7 %broadcast_select_fusion.1 = bf16[16,2,128,512]{3,2,1,0:T(8,128)(2,1)} fusion(bf16[16,2,128,512]{3,2,1,0:T(8,128)(2,1)} %gather_fusion.3, pred[16]{0:T(512)(128)(4,1)S(1)} %compare_and_fusion.1), kind=kLoop, calls=%fused_computation.17 | loop fusion | flops 2097152 | bytes 8388624 | tf_op jit(solution)/shard_map/jit(_take)/select_n | solution.py:85
  83.4 5.2 %all-to-all-start.1 = ((bf16[16,2,128,512]{3,2,1,0:T(8,128)(2,1)}), bf16[16,2,128,512]{3,2,1,0:T(8,128)(2,1)}, u32[]{:S(2)}, u32[]{:S(2)}) async-start(bf16[16,2,128,512]{3,2,1,0:T(8,128)(2,1)} %broadcast_select_fusion.1), calls=%async_computation.1 | async-start | bytes 8388608 | tf_op jit(solution)/shard_map/all_to_all | solution.py:86
  88.7 4.0 fusion.7
  94.6 9.3 %psum.29 = f32[128]{0:T(128)S(1)} all-reduce(f32[128]{0:T(128)S(1)} %multiply_reduce_fusion.1), channel_id=1, replica_groups=mesh['grp'=4,'kv'=4,'tp'=2] {'kv'}, use_global_device_ids=true, to_apply=%region_2.0 | all-reduce | flops 128 | bytes 1024 | tf_op jit(solution)/shard_map/psum | solution.py:161
  104.2 41.8 %all-reduce.4.cloned.1.call-done = f32[128,2048]{1,0:T(8,128)} async-done(((f32[128,2048]{1,0:T(8,128)}), f32[128,2048]{1,0:T(8,128)}) %all-reduce.4.cloned.1.call-update) | async-done | bytes 1048592 | tf_op jit(solution)/shard_map/psum | solution.py:161
  145.9 1.4 multiply_multiply_fusion
  148.0 1.3 gather_fusion
  149.4 2.5 fusion.34
  151.9 29.4 %all-to-all-done.1 = bf16[16,2,128,512]{3,2,1,0:T(8,128)(2,1)} async-done(((bf16[16,2,128,512]{3,2,1,0:T(8,128)(2,1)}), bf16[16,2,128,512]{3,2,1,0:T(8,128)(2,1)}, u32[]{:S(2)}, u32[]{:S(2)}) %all-to-all-start.1) | async-done | bytes 4194336 | tf_op jit(solution)/shard_map/all_to_all | solution.py:86
  181.3 5.0 %gather_fusion.4 = bf16[16,2,128,512]{3,2,1,0:T(8,128)(2,1)} fusion(bf16[16,2,128,512]{3,2,1,0:T(8,128)(2,1)} %all-to-all-done.1, s32[1024]{0:T(1024)S(1)} %pad_clamp_fusion), kind=kCustom, calls=%fused_computation.2.clone | custom fusion | bytes 8388672 | tf_op jit(solution)/shard_map/jit(_take)/gather | solution.py:90
  186.3 2.8 broadcast_select_fusion
  189.1 2.9 pad_maximum_fusion
  192.0 3.5 copy.122
  195.5 4.2 fusion.33
  200.2 1.8 exponential_select_fusion
  202.7 3.5 copy.130
  206.2 6.6 %fusion.13 = f32[24,4,4,128]{3,2,1,0:T(4,128)} fusion(bf16[24,128,4,128]{1,3,2,0:T(8,128)(2,1)S(1)} %bitcast.95, f32[24,4,4,128]{3,2,1,0:T(4,128)} %get-tuple-element.261, f32[24,4,4]{2,1,0:T(4,128)S(1)} %broadcast_select_fusion.3, pred[24,128]{1,0:T(8,128)(4,1)S(1)} %iota_compare_fusion), kind=kOutput, calls=%fused_computation.50 | convolution fusion | flops 75595776 | bytes 3543552 | tf_op jit(solution)/shard_map/ikgt,itkd->ikgd/dot_general | solution.py:120
  212.8 1.0 reshape.456
  214.0 1.0 copy.129
  215.0 1.7 convolution_add_fusion
  216.8 1.7 copy.135
  218.8 6.7 %copy.138 = bf16[4096,512]{1,0:T(8,128)(2,1)} copy(bf16[4096,512]{0,1:T(8,128)(2,1)} %bitcast.92) | data formatting | bytes 8388608 | tf_op jit(solution)/shard_map/dot_general | solution.py:182
  226.2 8.0 %all-gather = f32[512,16]{0,1:T(8,128)S(1)} all-gather(f32[128,16]{0,1:T(8,128)S(1)} %convolution_add_fusion.1), channel_id=2, replica_groups=mesh['grp'=4,'kv'=4,'tp'=2] {'kv'}, dimensions={0}, use_global_device_ids=true | all-gather | bytes 40960 | tf_op jit(solution)/shard_map/all_gather | solution.py:16
  234.3 8.2 %all_gather.12 = f32[4,128,16]{1,2,0:T(8,128)S(1)} all-gather(f32[1,128,16]{1,2,0:T(8,128)S(1)} %bitcast.104), channel_id=1, replica_groups=mesh['grp'=4,'kv'=4,'tp'=2] {'kv'}, dimensions={0}, use_global_device_ids=true | all-gather | bytes 40960 | tf_op jit(solution)/shard_map/all_gather | solution.py:16
  242.5 26.1 %all-gather.3.cloned.1.call-done = f32[4,128,16,128]{3,2,1,0:T(8,128)} async-done(((f32[1,128,16,128]{3,2,1,0:T(8,128)}), f32[4,128,16,128]{3,2,1,0:T(8,128)}) %all-gather.3.cloned.1.call-update) | async-done | bytes 4194320 | tf_op jit(solution)/shard_map/all_gather | solution.py:16
  268.7 1.3 slice_bitcast_fusion
  270.0 6.5 %while.19 = (s32[]{:T(128)}, f32[128,16]{0,1:T(8,128)S(1)}, f32[128,16]{0,1:T(8,128)S(1)}, f32[128,16,128]{2,1,0:T(8,128)S(1)}, f32[4,128,16]{1,2,0:T(8,128)S(1)...) while((s32[]{:T(128)}, f32[128,16]{0,1:T(8,128)S(1)}, ...), condition=%wide.region_14.16_spmd, body=%wide.region_13.15_spmd.sunk | while | flops 798725 | bytes 3276955 | solution.py:21
  270.2 1.9 fusion.48
  272.4 1.9 fusion.48
  274.5 1.9 fusion.48
  276.9 3.7 add_convert_fusion
  281.3 1.4 copy.141
  282.7 52.6 %all-reduce.6.cloned.1.call-done = bf16[128,4096]{1,0:T(8,128)(2,1)} async-done(((bf16[128,4096]{1,0:T(8,128)(2,1)}), bf16[128,4096]{1,0:T(8,128)(2,1)}) %all-reduce.6.cloned.1.call-update) | async-done | bytes 1048592 | tf_op jit(solution)/shard_map/psum | solution.py:192
  335.4 21.6 %all-reduce.8.cloned.1.call-done = bf16[128,4096]{1,0:T(8,128)(2,1)} async-done(((bf16[128,4096]{1,0:T(8,128)(2,1)}), bf16[128,4096]{1,0:T(8,128)(2,1)}) %all-reduce.8.cloned.1.call-update) | async-done | bytes 1048592 | tf_op jit(solution)/shard_map/psum | solution.py:191
  357.0 1.5 multiply_reduce_fusion
  358.5 7.7 %convolution_multiply_fusion.1 = f32[128,1792]{1,0:T(8,128)S(1)} fusion(bf16[4096,1792]{1,0:T(8,128)(2,1)} %param.26, f32[4096]{0:T(1024)S(1)} %copy-done.7, bf16[128,4096]{1,0:T(8,128)(2,1)} %all-reduce.8.cloned.1.call-done, f32[128]{0:T(128)S(1)} %add_rsqrt_fusion), kind=kOutput, calls=%fused_computation.22 | convolution fusion | flops 1880850432 | bytes 16663040 | tf_op jit(solution)/shard_map/dot_general | solution.py:197
  366.2 14.8 %convolution_convert_fusion = bf16[128,4096]{1,0:T(8,128)(2,1)} fusion(bf16[1792,4096]{1,0:T(8,128)(2,1)} %param.28, bf16[4096,1792]{1,0:T(8,128)(2,1)} %param.27, f32[128,1792]{1,0:T(8,128)S(1)} %convolution_multiply_fusion.1, f32[4096]{0:T(1024)S(1)} %copy-done.7, bf16[128,4096]{1,0:T(8,128)(2,1)S(1)} %copy-done, f32[128]{0:T(128)S(1)} %add_rsqrt_fusion), kind=kOutput, calls=%fused_computation.15 | convolution fusion | flops 3761799168 | bytes 32391680 | tf_op jit(solution)/shard_map/dot_general | solution.py:202
  381.0 4.7 %fusion.46 = bf16[1,16,2,128,512]{4,3,2,1,0:T(8,128)(2,1)} fusion(bf16[16,2,128,512]{3,2,1,0:T(8,128)(2,1)} %gather_fusion.4, pred[16]{0:T(512)(128)(4,1)S(1)} %get-tuple-element.246), kind=kLoop, calls=%fused_computation.127 | loop fusion | flops 2097152 | bytes 8388624 | tf_op jit(solution)/shard_map/broadcast_in_dim | solution.py:210
  385.9 32.5 %reduce-scatter.2.cloned.1.call-done = bf16[16,4096]{1,0:T(8,128)(2,1)} async-done(((bf16[128,4096]{1,0:T(8,128)(2,1)}), bf16[16,4096]{1,0:T(8,128)(2,1)}) %reduce-scatter.2.cloned.1.call-update) | async-done | bytes 131088 | tf_op jit(solution)/shard_map/reduce_scatter | solution.py:201
  418.3 1.6 add_convert_fusion.1
  (111 shorter events, 9.0 us)
Async XLA Ops:
  19.9 53.8 %all-to-all-start = ((bf16[16,2,128,512]{3,2,1,0:T(8,128)(2,1)}), bf16[16,2,128,512]{3,2,1,0:T(8,128)(2,1)}, u32[]{:S(2)}, u32[]{:S(2)}) async-start(bf16[16,2,128,512]{3,2,1,0:T(8,128)(2,1)} %broadcast_select_fusion.2), calls=%async_computation | async-start | bytes 8388608 | tf_op jit(solution)/shard_map/all_to_all | solution.py:70
  83.4 5.3 %copy-start.1 = (bf16[128,1024]{1,0:T(8,128)(2,1)S(1)}, bf16[128,1024]{1,0:T(8,128)(2,1)}, u32[]{:S(2)}) copy-start(bf16[128,1024]{1,0:T(8,128)(2,1)} %param.21) | copy-start | bytes 786436
  83.4 5.3 %copy-start.8 = (f32[1024]{0:T(1024)S(1)}, f32[1024]{0:T(1024)}, u32[]{:S(2)}) copy-start(f32[1024]{0:T(1024)} %param.22) | copy-start | bytes 12292
  83.4 97.9 %all-to-all-start.1 = ((bf16[16,2,128,512]{3,2,1,0:T(8,128)(2,1)}), bf16[16,2,128,512]{3,2,1,0:T(8,128)(2,1)}, u32[]{:S(2)}, u32[]{:S(2)}) async-start(bf16[16,2,128,512]{3,2,1,0:T(8,128)(2,1)} %broadcast_select_fusion.1), calls=%async_computation.1 | async-start | bytes 8388608 | tf_op jit(solution)/shard_map/all_to_all | solution.py:86
  88.6 4.2 copy-start.9
  88.6 4.2 copy-start.10
  88.6 4.5 %copy-start.5 = (bf16[128,2,512]{2,1,0:T(2,128)(2,1)S(1)}, bf16[128,2,512]{2,1,0:T(2,128)(2,1)}, u32[]{:S(2)}) copy-start(bf16[128,2,512]{2,1,0:T(2,128)(2,1)} %param.37) | copy-start | bytes 786436
  88.6 4.9 %copy-start.11 = (s32[1,16]{1,0:T(1,128)S(1)}, s32[1,16]{1,0:T(1,128)}, u32[]{:S(2)}) copy-start(s32[1,16]{1,0:T(1,128)} %param.36) | copy-start | bytes 196
  88.6 4.9 %copy-start.12 = (s32[1,8]{1,0:T(1,128)S(1)}, s32[1,8]{1,0:T(1,128)}, u32[]{:S(2)}) copy-start(s32[1,8]{1,0:T(1,128)} %param.32) | copy-start | bytes 100
  88.6 57.3 %all-reduce.4.cloned.1.call-start = ((), (), s32[]{:S(2)}) async-start(), calls=%async_computation.3 | async-start | bytes 2097152 | tf_op jit(solution)/shard_map/psum | solution.py:161
  92.7 176.0 %all-gather.3.cloned.1.call-start = ((), (), s32[]{:S(2)}) async-start(), calls=%async_computation.4 | async-start | bytes 5242880 | tf_op jit(solution)/shard_map/all_gather | solution.py:16
  186.3 2.9 copy-start.2
  202.0 0.7 copy-start.3
  218.5 116.9 %all-reduce.6.cloned.1.call-start = ((), (), s32[]{:S(2)}) async-start(), calls=%async_computation.5 | async-start | bytes 2097152 | tf_op jit(solution)/shard_map/psum | solution.py:192
  218.8 6.7 %copy-start.6 = (f32[24,4,4,128]{3,2,1,0:T(4,128)S(1)}, f32[24,4,4,128]{3,2,1,0:T(4,128)}, u32[]{:S(2)}) copy-start(f32[24,4,4,128]{3,2,1,0:T(4,128)} %get-tuple-element.261) | copy-start | bytes 589828
  218.8 15.4 %copy-start.4 = (f32[128,4,4]{2,1,0:T(4,128)S(1)}, f32[128,4,4]{2,1,0:T(4,128)}, u32[]{:S(2)}) copy-start(f32[128,4,4]{2,1,0:T(4,128)} %copy-done.3) | copy-start | bytes 24580
  280.6 77.9 %copy-start.7 = (f32[4096]{0:T(1024)S(1)}, f32[4096]{0:T(1024)}, u32[]{:S(2)}) copy-start(f32[4096]{0:T(1024)} %param.23) | copy-start | bytes 49156
  282.7 74.3 %all-reduce.8.cloned.1.call-start = ((), (), s32[]{:S(2)}) async-start(), calls=%async_computation.6 | async-start | bytes 2097152 | tf_op jit(solution)/shard_map/psum | solution.py:191
  335.3 83.0 %reduce-scatter.2.cloned.1.call-start = ((), (), s32[]{:S(2)}) async-start(), calls=%async_computation.7 | async-start | bytes 1179648 | tf_op jit(solution)/shard_map/reduce_scatter | solution.py:201
  358.5 7.7 %copy-start = (bf16[128,4096]{1,0:T(8,128)(2,1)S(1)}, bf16[128,4096]{1,0:T(8,128)(2,1)}, u32[]{:S(2)}) copy-start(bf16[128,4096]{1,0:T(8,128)(2,1)} %all-reduce.8.cloned.1.call-done) | copy-start | bytes 3145732
Sparse Core Ops, SparseCore 0:
  92.8 53.0 all-reduce.3
  218.6 50.0 all-gather.2
  282.8 52.4 all-reduce.5
  337.5 19.4 all-reduce.7
  381.1 37.1 reduce-scatter.1
